TPU v7x, 32 devices: a whole 2x2x4 slice. The times are simulated.
32 devices in a mesh: gx: 4 (over y, x), gy: 2 (over core), gz: 4 (over z).
Axes of the slice: x: 2, y: 2, z: 4, core: 2. Of those that a mesh axis runs over, the one named last changes fastest.
Arguments:
- star_residual: bfloat16 [128, 64, 1152], P(('gx', 'gy', 'gz')), may hold values from -6 to 6
- patch_inverse: bfloat16 [128, 1152, 1152], P(('gx', 'gy', 'gz')), may hold values from -0.1875 to 0.1875
- block_owner: int32 [128, 9], P(('gx', 'gy', 'gz')), may hold values from 0 to 31, as said below
- block_slot: int32 [128, 9], P(('gx', 'gy', 'gz')), may hold values from 0 to 1, as said below
- recv_target: int32 [32, 27, 2], P(('gx', 'gy', 'gz')), may hold values from -1 to 7, as said below
Outputs:
- owned_sum: float32 [256, 64, 128], P(('gx', 'gy', 'gz'))
- combined: float32 [128, 9, 64, 128], P(('gx', 'gy', 'gz'))
Inputs may be any that keep to these rules, and one draw needn't show every extreme that they name: `block_owner`: each block's owner is the block's own partition or one whose coordinate differs by at most one step along each of the three mesh axes, counted with wrap-around. `block_slot`: blocks of one partition that have the same owner have distinct slots; in every partition some owner receives exactly 2 of its blocks. `recv_target`: every slot that a block uses maps to an owned block of its owner; slots that no block uses hold -1.
All inputs are finite; a program needn't handle non-finite values.
Results may differ from a plain program's by a relative error of at most 0.0003.
Values sent between devices are 32-bit elements; how exact they have to be, the bound alone decides.
A program may use at most 64 MiB of HBM per device.

v0:
```python
import jax
import jax.numpy as jnp
from jax import lax
from jax.sharding import PartitionSpec as P

OWNB = 8


def from_behind(array, axis, by):
    length = lax.axis_size(axis)
    return lax.ppermute(array, axis, [(i, (i + by) % length) for i in range(length)])


def axis_code(far_index, near_index, extent):
    distance = (far_index - near_index) % extent
    return jnp.where(distance == 0, 1, jnp.where(distance == 1, 2, 0)).astype(jnp.int32)


def offset_code(far_ids, near_ids, extents):
    size_x, size_y, size_z = extents
    code_x = axis_code(far_ids // (size_y * size_z), near_ids // (size_y * size_z), size_x)
    code_y = axis_code(far_ids // size_z % size_y, near_ids // size_z % size_y, size_y)
    code_z = axis_code(far_ids % size_z, near_ids % size_z, size_z)
    return 9 * code_x + 3 * code_y + code_z


def one_hot(indices, count):
    return (indices[:, None] == jnp.arange(count, dtype=jnp.int32)[None, :]).astype(jnp.float32)


def spread(placing, values):
    return jnp.einsum("nk,nf->kf", placing, values, precision=lax.Precision.HIGHEST)


def collect(placing, values):
    return jnp.einsum("nk,kf->nf", placing, values, precision=lax.Precision.HIGHEST)


def move_layers(buffer, dim, upper_move, lower_move):
    lower = lax.index_in_dim(buffer, 0, dim, keepdims=True)
    middle = lax.index_in_dim(buffer, 1, dim, keepdims=True)
    upper = lax.index_in_dim(buffer, 2, dim, keepdims=True)
    return jnp.concatenate([lower_move(lower), middle, upper_move(upper)], axis=dim)


def on_device(star_residual, patch_inverse, block_owner, block_slot, recv_target):
    extents = (lax.axis_size("gx"), lax.axis_size("gy"), lax.axis_size("gz"))
    my_index = lax.axis_index(("gx", "gy", "gz"))
    patch_count, rhs_count, patch_order = star_residual.shape
    block_count = block_owner.shape[1]
    block_width = patch_order // block_count
    capacity = recv_target.shape[2]
    feature = rhs_count * block_width
    inverse_blocks = patch_inverse.reshape(patch_count, block_count, block_width, patch_order)
    contribution = jnp.einsum(
        "prj,pbwj->pbrw", star_residual, inverse_blocks, preferred_element_type=jnp.float32
    )
    blocks = contribution.reshape(patch_count * block_count, feature)
    owner_ids = block_owner.reshape(-1)
    slot_ids = block_slot.reshape(-1)
    target_table = recv_target[0]
    send_code = offset_code(owner_ids, my_index, extents)
    placing = one_hot(send_code * capacity + slot_ids, 27 * capacity)
    outgoing = spread(placing, blocks).reshape(3, 3, 3, capacity, feature)
    arrived = move_layers(
        outgoing, 0, lambda v: from_behind(v, "gx", 1), lambda v: from_behind(v, "gx", -1)
    )
    arrived = move_layers(
        arrived, 1, lambda v: from_behind(v, "gy", 1), lambda v: from_behind(v, "gy", -1)
    )
    arrived = move_layers(
        arrived, 2, lambda v: from_behind(v, "gz", 1), lambda v: from_behind(v, "gz", -1)
    )
    arrived = arrived.reshape(27 * capacity, feature)
    picking = one_hot(target_table.reshape(-1), OWNB)
    owned_total = spread(picking, arrived)
    answer = collect(picking, owned_total).reshape(3, 3, 3, capacity, feature)
    returned = move_layers(
        answer, 0, lambda v: from_behind(v, "gx", -1), lambda v: from_behind(v, "gx", 1)
    )
    returned = move_layers(
        returned, 1, lambda v: from_behind(v, "gy", -1), lambda v: from_behind(v, "gy", 1)
    )
    returned = move_layers(
        returned, 2, lambda v: from_behind(v, "gz", -1), lambda v: from_behind(v, "gz", 1)
    )
    combined_blocks = collect(placing, returned.reshape(27 * capacity, feature))
    owned_sum = owned_total.reshape(OWNB, rhs_count, block_width)
    combined = combined_blocks.reshape(patch_count, block_count, rhs_count, block_width)
    return (owned_sum, combined)


def solution(mesh):
    placed = (
        P(("gx", "gy", "gz"), None, None),
        P(("gx", "gy", "gz"), None, None),
        P(("gx", "gy", "gz"), None),
        P(("gx", "gy", "gz"), None),
        P(("gx", "gy", "gz"), None, None),
    )
    return jax.shard_map(
        on_device,
        mesh=mesh,
        in_specs=placed,
        out_specs=(P(("gx", "gy", "gz"), None, None), P(("gx", "gy", "gz"), None, None, None)),
        check_vma=False,
    )
```

profile of v0, /device:TPU:1, one launch (start us, length us, event | category | flops | bytes accessed | tf_op | source)
XLA Modules:
  0.0 153.6 jit_solution(4059164150423159236)
XLA Ops:
  2.3 6.0 %fusion.3 = f32[4,9,128,64]{2,3,1,0:T(8,128)S(1)} fusion(bf16[4,9,128,1152]{3,2,1,0:T(8,128)(2,1)} %bitcast.32, bf16[4,64,1152]{2,1,0:T(8,128)(2,1)S(1)} %copy-done), kind=kOutput, calls=%fused_computation.8 | convolution fusion | flops 679477248 | bytes 12386304 | tf_op jit(solution)/shard_map/prj,pbwj->pbrw/dot_general | solution.py:55
  9.3 1.0 fusion.9
  10.5 1.2 slice.73
  11.6 3.0 %collective-permute-start = (f32[1,3,3,2,8192]{4,3,2,1,0:T(2,128)}, f32[1,3,3,2,8192]{4,3,2,1,0:T(2,128)S(1)}, u32[]{:S(2)}, u32[]{:S(2)}) collective-permute-start(f32[1,3,3,2,8192]{4,3,2,1,0:T(2,128)} %slice.73), channel_id=1, source_target_pairs={{0,24},{8,0},{16,8},{24,16},{1,25},{9,1},{17,9},{25,17},{2,26},{10... | collective-permute-start | bytes 1769480 | tf_op jit(solution)/shard_map/ppermute | solution.py:11
  14.6 1.2 slice.77
  16.1 10.8 %collective-permute-done = f32[1,3,3,2,8192]{4,3,2,1,0:T(2,128)S(1)} collective-permute-done((f32[1,3,3,2,8192]{4,3,2,1,0:T(2,128)}, f32[1,3,3,2,8192]{4,3,2,1,0:T(2,128)S(1)}, u32[]{:S(2)}, u32[]{:S(2)}) %collective-permute-start) | collective-permute-done | bytes 589856 | tf_op jit(solution)/shard_map/ppermute | solution.py:11
  27.1 13.4 %collective-permute-done.1 = f32[1,3,3,2,8192]{4,3,2,1,0:T(2,128)S(1)} collective-permute-done((f32[1,3,3,2,8192]{4,3,2,1,0:T(2,128)}, f32[1,3,3,2,8192]{4,3,2,1,0:T(2,128)S(1)}, u32[]{:S(2)}, u32[]{:S(2)}) %collective-permute-start.1) | collective-permute-done | bytes 589856 | tf_op jit(solution)/shard_map/ppermute | solution.py:11
  40.7 1.6 %collective-permute-start.2 = (f32[3,1,3,2,8192]{4,3,2,1,0:T(2,128)S(1)}, f32[3,1,3,2,8192]{4,3,2,1,0:T(2,128)S(1)}, u32[]{:S(2)}, u32[]{:S(2)}) collective-permute-start(f32[3,1,3,2,8192]{4,3,2,1,0:T(2,128)S(1)} %get-tuple-element.21), channel_id=1, source_target_pairs={{0,4},{4,0},{1,5},{5,1},{2,6},{6,2},{3,7},{7,3},{8,12},{12,8},{9,1... | collective-permute-start | bytes 1769480 | tf_op jit(solution)/shard_map/ppermute | solution.py:11
  42.4 1.6 %collective-permute-done.2 = f32[3,1,3,2,8192]{4,3,2,1,0:T(2,128)S(1)} collective-permute-done((f32[3,1,3,2,8192]{4,3,2,1,0:T(2,128)S(1)}, f32[3,1,3,2,8192]{4,3,2,1,0:T(2,128)S(1)}, u32[]{:S(2)}, u32[]{:S(2)}) %collective-permute-start.2) | collective-permute-done | bytes 589856 | tf_op jit(solution)/shard_map/ppermute | solution.py:11
  44.8 1.3 pad_maximum_fusion
  46.2 3.4 %collective-permute-start.4 = (f32[3,3,1,2,8192]{4,3,2,1,0:T(2,128)S(1)}, f32[3,3,1,2,8192]{4,3,2,1,0:T(2,128)S(1)}, u32[]{:S(2)}, u32[]{:S(2)}) collective-permute-start(f32[3,3,1,2,8192]{4,3,2,1,0:T(2,128)S(1)} %get-tuple-element.18), channel_id=1, source_target_pairs={{0,3},{1,0},{2,1},{3,2},{4,7},{5,4},{6,5},{7,6},{8,11},{9,8},{10,9... | collective-permute-start | bytes 1769480 | tf_op jit(solution)/shard_map/ppermute | solution.py:11
  51.0 11.0 %collective-permute-done.4 = f32[3,3,1,2,8192]{4,3,2,1,0:T(2,128)S(1)} collective-permute-done((f32[3,3,1,2,8192]{4,3,2,1,0:T(2,128)S(1)}, f32[3,3,1,2,8192]{4,3,2,1,0:T(2,128)S(1)}, u32[]{:S(2)}, u32[]{:S(2)}) %collective-permute-start.4) | collective-permute-done | bytes 589856 | tf_op jit(solution)/shard_map/ppermute | solution.py:11
  61.9 13.5 %collective-permute-done.5 = f32[3,3,1,2,8192]{4,3,2,1,0:T(2,128)S(1)} collective-permute-done((f32[3,3,1,2,8192]{4,3,2,1,0:T(2,128)S(1)}, f32[3,3,1,2,8192]{4,3,2,1,0:T(2,128)S(1)}, u32[]{:S(2)}, u32[]{:S(2)}) %collective-permute-start.5) | collective-permute-done | bytes 589856 | tf_op jit(solution)/shard_map/ppermute | solution.py:11
  75.4 2.2 %pad_maximum_fusion.1 = f32[3,3,3,2,8192]{4,3,2,1,0:T(2,128)} fusion(f32[3,3,1,2,8192]{4,3,2,1,0:T(2,128)S(1)} %collective-permute-done.5, f32[3,3,1,2,8192]{4,3,2,1,0:T(2,128)S(1)} %get-tuple-element.20, f32[3,3,1,2,8192]{4,3,2,1,0:T(2,128)S(1)} %collective-permute-done.4), kind=kLoop, calls=%fused_computation.5 | loop fusion | flops 884736 | bytes 3538944 | tf_op jit(solution)/shard_map/concatenate | solution.py:43
  77.6 2.5 %reshape.190 = f32[54,8192]{1,0:T(8,128)S(1)} reshape(f32[3,3,3,2,8192]{4,3,2,1,0:T(2,128)} %pad_maximum_fusion.1) | data formatting | bytes 3538944 | tf_op jit(solution)/shard_map/reshape | solution.py:74
  82.0 1.2 slice.85
  83.2 1.2 collective-permute-start.6
  84.4 1.2 slice.89
  85.9 1.4 collective-permute-start.7
  87.3 10.6 %collective-permute-done.6 = f32[1,3,3,2,8192]{4,3,2,1,0:T(2,128)S(1)} collective-permute-done((f32[1,3,3,2,8192]{4,3,2,1,0:T(2,128)}, f32[1,3,3,2,8192]{4,3,2,1,0:T(2,128)S(1)}, u32[]{:S(2)}, u32[]{:S(2)}) %collective-permute-start.6) | collective-permute-done | bytes 589856 | tf_op jit(solution)/shard_map/ppermute | solution.py:11
  98.1 11.6 %collective-permute-done.7 = f32[1,3,3,2,8192]{4,3,2,1,0:T(2,128)S(1)} collective-permute-done((f32[1,3,3,2,8192]{4,3,2,1,0:T(2,128)}, f32[1,3,3,2,8192]{4,3,2,1,0:T(2,128)S(1)}, u32[]{:S(2)}, u32[]{:S(2)}) %collective-permute-start.7) | collective-permute-done | bytes 589856 | tf_op jit(solution)/shard_map/ppermute | solution.py:11
  109.9 2.1 %collective-permute-start.8 = (f32[3,1,3,2,8192]{4,3,2,1,0:T(2,128)S(1)}, f32[3,1,3,2,8192]{4,3,2,1,0:T(2,128)S(1)}, u32[]{:S(2)}, u32[]{:S(2)}) collective-permute-start(f32[3,1,3,2,8192]{4,3,2,1,0:T(2,128)S(1)} %get-tuple-element.15), channel_id=1, source_target_pairs={{0,4},{4,0},{1,5},{5,1},{2,6},{6,2},{3,7},{7,3},{8,12},{12,8},{9,1... | collective-permute-start | bytes 1769480 | tf_op jit(solution)/shard_map/ppermute | solution.py:11
  112.1 1.6 %collective-permute-done.8 = f32[3,1,3,2,8192]{4,3,2,1,0:T(2,128)S(1)} collective-permute-done((f32[3,1,3,2,8192]{4,3,2,1,0:T(2,128)S(1)}, f32[3,1,3,2,8192]{4,3,2,1,0:T(2,128)S(1)}, u32[]{:S(2)}, u32[]{:S(2)}) %collective-permute-start.8) | collective-permute-done | bytes 589856 | tf_op jit(solution)/shard_map/ppermute | solution.py:11
  114.5 1.3 pad_maximum_fusion.2
  115.9 1.4 collective-permute-start.10
  117.3 1.9 %collective-permute-start.11 = (f32[3,3,1,2,8192]{4,3,2,1,0:T(2,128)S(1)}, f32[3,3,1,2,8192]{4,3,2,1,0:T(2,128)S(1)}, u32[]{:S(2)}, u32[]{:S(2)}) collective-permute-start(f32[3,3,1,2,8192]{4,3,2,1,0:T(2,128)S(1)} %get-tuple-element.13), channel_id=1, source_target_pairs={{0,3},{1,0},{2,1},{3,2},{4,7},{5,4},{6,5},{7,6},{8,11},{9,8},{10,9... | collective-permute-start | bytes 1769480 | tf_op jit(solution)/shard_map/ppermute | solution.py:11
  120.0 12.3 %collective-permute-done.10 = f32[3,3,1,2,8192]{4,3,2,1,0:T(2,128)S(1)} collective-permute-done((f32[3,3,1,2,8192]{4,3,2,1,0:T(2,128)S(1)}, f32[3,3,1,2,8192]{4,3,2,1,0:T(2,128)S(1)}, u32[]{:S(2)}, u32[]{:S(2)}) %collective-permute-start.10) | collective-permute-done | bytes 589856 | tf_op jit(solution)/shard_map/ppermute | solution.py:11
  132.3 12.4 %collective-permute-done.11 = f32[3,3,1,2,8192]{4,3,2,1,0:T(2,128)S(1)} collective-permute-done((f32[3,3,1,2,8192]{4,3,2,1,0:T(2,128)S(1)}, f32[3,3,1,2,8192]{4,3,2,1,0:T(2,128)S(1)}, u32[]{:S(2)}, u32[]{:S(2)}) %collective-permute-start.11) | collective-permute-done | bytes 589856 | tf_op jit(solution)/shard_map/ppermute | solution.py:11
  144.8 2.2 %pad_maximum_fusion.3 = f32[3,3,3,2,8192]{4,3,2,1,0:T(2,128)} fusion(f32[3,3,1,2,8192]{4,3,2,1,0:T(2,128)S(1)} %collective-permute-done.11, f32[3,3,1,2,8192]{4,3,2,1,0:T(2,128)S(1)} %get-tuple-element.14, f32[3,3,1,2,8192]{4,3,2,1,0:T(2,128)S(1)} %collective-permute-done.10), kind=kLoop, calls=%fused_computation.7 | loop fusion | flops 884736 | bytes 3538944 | tf_op jit(solution)/shard_map/concatenate | solution.py:43
  146.9 2.5 %reshape.192 = f32[54,8192]{1,0:T(8,128)S(1)} reshape(f32[3,3,3,2,8192]{4,3,2,1,0:T(2,128)} %pad_maximum_fusion.3) | data formatting | bytes 3538944 | tf_op jit(solution)/shard_map/reshape | solution.py:87
  150.0 2.2 %fusion = f32[4,9,64,128]{3,1,2,0:T(8,128)S(1)} fusion(f32[64,128,54]{1,0,2:T(8,128)S(1)} %slice_bitcast_fusion, s32[4,9]{1,0:T(4,128)S(1)} %multiply_add_fusion), kind=kOutput, calls=%fused_computation | convolution fusion | flops 191104928 | bytes 2949264 | tf_op jit(solution)/shard_map/nk,kf->nf/dot_general | solution.py:36
  152.3 1.4 copy.13
  (41 shorter events, 10.8 us)
Async XLA Ops:
  0.6 1.6 %copy-start = (bf16[4,64,1152]{2,1,0:T(8,128)(2,1)S(1)}, bf16[4,64,1152]{2,1,0:T(8,128)(2,1)}, u32[]{:S(2)}) copy-start(bf16[4,64,1152]{2,1,0:T(8,128)(2,1)} %param.5) | copy-start | bytes 1769476
  11.6 15.3 %collective-permute-start = (f32[1,3,3,2,8192]{4,3,2,1,0:T(2,128)}, f32[1,3,3,2,8192]{4,3,2,1,0:T(2,128)S(1)}, u32[]{:S(2)}, u32[]{:S(2)}) collective-permute-start(f32[1,3,3,2,8192]{4,3,2,1,0:T(2,128)} %slice.73), channel_id=1, source_target_pairs={{0,24},{8,0},{16,8},{24,16},{1,25},{9,1},{17,9},{25,17},{2,26},{10... | collective-permute-start | bytes 1769480 | tf_op jit(solution)/shard_map/ppermute | solution.py:11
  15.8 24.7 %collective-permute-start.1 = (f32[1,3,3,2,8192]{4,3,2,1,0:T(2,128)}, f32[1,3,3,2,8192]{4,3,2,1,0:T(2,128)S(1)}, u32[]{:S(2)}, u32[]{:S(2)}) collective-permute-start(f32[1,3,3,2,8192]{4,3,2,1,0:T(2,128)} %slice.77), channel_id=1, source_target_pairs={{0,8},{8,16},{16,24},{24,0},{1,9},{9,17},{17,25},{25,1},{2,10},{10... | collective-permute-start | bytes 1769480 | tf_op jit(solution)/shard_map/ppermute | solution.py:11
  40.7 3.2 %collective-permute-start.2 = (f32[3,1,3,2,8192]{4,3,2,1,0:T(2,128)S(1)}, f32[3,1,3,2,8192]{4,3,2,1,0:T(2,128)S(1)}, u32[]{:S(2)}, u32[]{:S(2)}) collective-permute-start(f32[3,1,3,2,8192]{4,3,2,1,0:T(2,128)S(1)} %get-tuple-element.21), channel_id=1, source_target_pairs={{0,4},{4,0},{1,5},{5,1},{2,6},{6,2},{3,7},{7,3},{8,12},{12,8},{9,1... | collective-permute-start | bytes 1769480 | tf_op jit(solution)/shard_map/ppermute | solution.py:11
  42.3 2.5 %collective-permute-start.3 = (f32[3,1,3,2,8192]{4,3,2,1,0:T(2,128)S(1)}, f32[3,1,3,2,8192]{4,3,2,1,0:T(2,128)S(1)}, u32[]{:S(2)}, u32[]{:S(2)}) collective-permute-start(f32[3,1,3,2,8192]{4,3,2,1,0:T(2,128)S(1)} %get-tuple-element.22), channel_id=1, source_target_pairs={{0,4},{4,0},{1,5},{5,1},{2,6},{6,2},{3,7},{7,3},{8,12},{12,8},{9,1... | collective-permute-start | bytes 1769480 | tf_op jit(solution)/shard_map/ppermute | solution.py:11
  46.2 15.7 %collective-permute-start.4 = (f32[3,3,1,2,8192]{4,3,2,1,0:T(2,128)S(1)}, f32[3,3,1,2,8192]{4,3,2,1,0:T(2,128)S(1)}, u32[]{:S(2)}, u32[]{:S(2)}) collective-permute-start(f32[3,3,1,2,8192]{4,3,2,1,0:T(2,128)S(1)} %get-tuple-element.18), channel_id=1, source_target_pairs={{0,3},{1,0},{2,1},{3,2},{4,7},{5,4},{6,5},{7,6},{8,11},{9,8},{10,9... | collective-permute-start | bytes 1769480 | tf_op jit(solution)/shard_map/ppermute | solution.py:11
  49.6 25.9 %collective-permute-start.5 = (f32[3,3,1,2,8192]{4,3,2,1,0:T(2,128)S(1)}, f32[3,3,1,2,8192]{4,3,2,1,0:T(2,128)S(1)}, u32[]{:S(2)}, u32[]{:S(2)}) collective-permute-start(f32[3,3,1,2,8192]{4,3,2,1,0:T(2,128)S(1)} %get-tuple-element.19), channel_id=1, source_target_pairs={{0,1},{1,2},{2,3},{3,0},{4,5},{5,6},{6,7},{7,4},{8,9},{9,10},{10,1... | collective-permute-start | bytes 1769480 | tf_op jit(solution)/shard_map/ppermute | solution.py:11
  77.6 2.5 %copy-start.3 = (s32[54]{0:T(128)S(1)}, s32[54]{0:T(128)}, u32[]{:S(2)}) copy-start(s32[54]{0:T(128)} %eq.119) | copy-start | bytes 652
  83.2 14.8 %collective-permute-start.6 = (f32[1,3,3,2,8192]{4,3,2,1,0:T(2,128)}, f32[1,3,3,2,8192]{4,3,2,1,0:T(2,128)S(1)}, u32[]{:S(2)}, u32[]{:S(2)}) collective-permute-start(f32[1,3,3,2,8192]{4,3,2,1,0:T(2,128)} %slice.85), channel_id=1, source_target_pairs={{0,8},{8,16},{16,24},{24,0},{1,9},{9,17},{17,25},{25,1},{2,10},{10... | collective-permute-start | bytes 1769480 | tf_op jit(solution)/shard_map/ppermute | solution.py:11
  85.9 23.7 %collective-permute-start.7 = (f32[1,3,3,2,8192]{4,3,2,1,0:T(2,128)}, f32[1,3,3,2,8192]{4,3,2,1,0:T(2,128)S(1)}, u32[]{:S(2)}, u32[]{:S(2)}) collective-permute-start(f32[1,3,3,2,8192]{4,3,2,1,0:T(2,128)} %slice.89), channel_id=1, source_target_pairs={{0,24},{8,0},{16,8},{24,16},{1,25},{9,1},{17,9},{25,17},{2,26},{10... | collective-permute-start | bytes 1769480 | tf_op jit(solution)/shard_map/ppermute | solution.py:11
  109.9 3.8 %collective-permute-start.8 = (f32[3,1,3,2,8192]{4,3,2,1,0:T(2,128)S(1)}, f32[3,1,3,2,8192]{4,3,2,1,0:T(2,128)S(1)}, u32[]{:S(2)}, u32[]{:S(2)}) collective-permute-start(f32[3,1,3,2,8192]{4,3,2,1,0:T(2,128)S(1)} %get-tuple-element.15), channel_id=1, source_target_pairs={{0,4},{4,0},{1,5},{5,1},{2,6},{6,2},{3,7},{7,3},{8,12},{12,8},{9,1... | collective-permute-start | bytes 1769480 | tf_op jit(solution)/shard_map/ppermute | solution.py:11
  112.0 2.5 %collective-permute-start.9 = (f32[3,1,3,2,8192]{4,3,2,1,0:T(2,128)S(1)}, f32[3,1,3,2,8192]{4,3,2,1,0:T(2,128)S(1)}, u32[]{:S(2)}, u32[]{:S(2)}) collective-permute-start(f32[3,1,3,2,8192]{4,3,2,1,0:T(2,128)S(1)} %get-tuple-element.16), channel_id=1, source_target_pairs={{0,4},{4,0},{1,5},{5,1},{2,6},{6,2},{3,7},{7,3},{8,12},{12,8},{9,1... | collective-permute-start | bytes 1769480 | tf_op jit(solution)/shard_map/ppermute | solution.py:11
  115.8 3.5 %copy-start.1 = (s32[4,9]{1,0:T(4,128)S(1)}, s32[4,9]{1,0:T(4,128)}, u32[]{:S(2)}) copy-start(s32[4,9]{1,0:T(4,128)} %param.8) | copy-start | bytes 436
  115.8 3.5 %copy-start.2 = (s32[4,9]{1,0:T(4,128)S(1)}, s32[4,9]{1,0:T(4,128)}, u32[]{:S(2)}) copy-start(s32[4,9]{1,0:T(4,128)} %param.7) | copy-start | bytes 436
  115.9 16.4 %collective-permute-start.10 = (f32[3,3,1,2,8192]{4,3,2,1,0:T(2,128)S(1)}, f32[3,3,1,2,8192]{4,3,2,1,0:T(2,128)S(1)}, u32[]{:S(2)}, u32[]{:S(2)}) collective-permute-start(f32[3,3,1,2,8192]{4,3,2,1,0:T(2,128)S(1)} %get-tuple-element.12), channel_id=1, source_target_pairs={{0,1},{1,2},{2,3},{3,0},{4,5},{5,6},{6,7},{7,4},{8,9},{9,10},{10,1... | collective-permute-start | bytes 1769480 | tf_op jit(solution)/shard_map/ppermute | solution.py:11
  117.3 27.4 %collective-permute-start.11 = (f32[3,3,1,2,8192]{4,3,2,1,0:T(2,128)S(1)}, f32[3,3,1,2,8192]{4,3,2,1,0:T(2,128)S(1)}, u32[]{:S(2)}, u32[]{:S(2)}) collective-permute-start(f32[3,3,1,2,8192]{4,3,2,1,0:T(2,128)S(1)} %get-tuple-element.13), channel_id=1, source_target_pairs={{0,3},{1,0},{2,1},{3,2},{4,7},{5,4},{6,5},{7,6},{8,11},{9,8},{10,9... | collective-permute-start | bytes 1769480 | tf_op jit(solution)/shard_map/ppermute | solution.py:11
where the time goes:
time: 155 us; the launch traced here: 154 us
  waiting for transfers between devices  100 us (65%)
  local copies, waits for them, and re-layouts  18.3 us (12%)
  starting transfers between devices  16.2 us (10%)
  matrix products  10.9 us (7%)
  other arithmetic  6.95 us (4%)
    ppermute x12, waiting for transfers between devices, from_behind(): lax.ppermute(array, axis, [(i, (i + by) % length) for i in range(length)])  100 us
    ppermute x12, starting transfers between devices, from_behind(): lax.ppermute(array, axis, [(i, (i + by) % length) for i in range(length)])  16.2 us
    concatenate x4, other arithmetic, move_layers(): jnp.concatenate([lower_move(lower), middle, upper_move(upper)], axis=dim)  6.88 us
    dot_general x1, matrix products, on_device(): jnp.einsum('prj,pbwj->pbrw', star_residual, inverse_blocks, preferred_ele...  5.98 us
    unnamed x18, local copies, waits for them, and re-layouts  4.42 us
    dot_general x2, matrix products, collect(): jnp.einsum('nk,kf->nf', placing, values, precision=lax.Precision.HIGHEST)  3.17 us
  transfers between devices with their start and end apart: 12, of which 12 were waited for; matrix products, arithmetic and copies ran while one was open for 4% of the time, Pallas kernels for 0%

commit v1 on v0

v1 whole, which is shorter than its diff:
```python
import functools

import jax
import jax.numpy as jnp
from jax import lax
from jax.experimental import pallas as pl
from jax.experimental.pallas import tpu as pltpu
from jax.sharding import PartitionSpec as P

OWNB = 8
CHUNKS = 2
MESH = pl.DeviceIdType.MESH


def offsets(extent):
    return [0, 1, -1][: min(extent, 3)]


def offset_index(far, near, extent):
    distance = (far - near) % extent
    return jnp.where(distance <= 1, distance, 2).astype(jnp.int32)


def code_of(offset):
    return offset + 1


def kernel(cfg, src_ref, key_ref, table_ref, star_ref, inv_hbm, owned_ref, comb_ref,
           star, inv, sent, came, tgt_out, tgt, pd, px, ry, rx, own, g1, g2, ans, back,
           load_sem, tgt_send, tgt_recv, a_send, a_recv, y_send, y_recv, x_send, x_recv,
           g_send, g_recv, h_send, h_recv, b_send, b_recv):
    nx, ny, nz, chunks, block_count, capacity = cfg
    gx, gy, gz = lax.axis_index("gx"), lax.axis_index("gy"), lax.axis_index("gz")
    patch_count = inv_hbm.shape[0] // block_count
    total = inv_hbm.shape[0]
    rows = came.shape[2]
    lanes = came.shape[3]
    pairs = [(dy, dz) for dy in offsets(ny) for dz in offsets(nz)]
    count = len(pairs)
    far = sorted(range(1, count), key=lambda q: pairs[q][1] == 0)
    near_x = (gx + 1 - 2 * (gx % 2), gy, gz)
    near_y = ((gx + 2) % 4, gy, gz)
    corner = (3 - gx, gy, gz)

    def ahead(q):
        return (gx, (gy + pairs[q][0] + ny) % ny, (gz + pairs[q][1] + nz) % nz)

    def behind(q):
        return (gx, (gy - pairs[q][0] + ny) % ny, (gz - pairs[q][1] + nz) % nz)

    loads = [pltpu.make_async_copy(star_ref, star, load_sem.at[patch_count])]
    for p in range(patch_count):
        part = pl.ds(p * block_count, block_count)
        loads.append(pltpu.make_async_copy(inv_hbm.at[part], inv.at[part], load_sem.at[p]))
    for load in loads:
        load.start()

    barrier = pltpu.get_barrier_semaphore()
    greeted = [ahead(q) for q in range(1, count)] + [near_x, near_y, corner]
    for device in greeted:
        pl.semaphore_signal(barrier, inc=1, device_id=device, device_id_type=MESH)

    parity = gx % 2
    for role in range(3):
        code_x = (1, 2 * parity, 2 - 2 * parity)[role]
        held = tgt if role == 0 else tgt_out
        for q in range(count):
            code = 9 * code_x + 3 * code_of(pairs[q][0]) + code_of(pairs[q][1])
            for s in range(capacity):
                i = q * capacity + s
                held[role, i:i + 1, :] = jnp.full((1, lanes), table_ref[0, code, s], jnp.int32)

    pl.semaphore_wait(barrier, len(greeted))

    sends = []

    def remote(source, target, send_sem, recv_sem, device):
        copy = pltpu.make_async_remote_copy(
            src_ref=source, dst_ref=target, send_sem=send_sem, recv_sem=recv_sem,
            device_id=device, device_id_type=MESH)
        return copy

    def launch(copy):
        copy.start()
        sends.append(copy)
        return copy

    tgt_copies = {}
    for role, device in ((1, near_x), (2, corner)):
        tgt_copies[role] = launch(remote(
            tgt_out.at[role], tgt.at[role], tgt_send.at[role - 1], tgt_recv.at[role - 1], device))

    def slot(q, role):
        return (q * 3 + role) * capacity

    def part(ref, c, q, role):
        return ref.at[c, pl.ds(slot(q, role), capacity)]

    for load in loads:
        load.wait()

    a_copies = {}
    for role in (2, 1, 0):
        for q in far + [0]:
            held = came if q == 0 else sent
            for s in range(capacity):
                k = slot(q, role) + s
                n = src_ref[k]
                block = lax.dot_general(
                    star[n // block_count], inv[n], (((1,), (1,)), ((), ())),
                    preferred_element_type=jnp.float32)
                for c in range(chunks):
                    held[c, k] = block[c * rows:(c + 1) * rows]
            if q:
                a_copies[q, role, 0] = launch(remote(
                    part(sent, 0, q, role), part(came, 0, q, role),
                    a_send.at[q, role, 0], a_recv.at[q, role, 0], ahead(q)))
        for c in range(1, chunks):
            for q in far:
                a_copies[q, role, c] = launch(remote(
                    part(sent, c, q, role), part(came, c, q, role),
                    a_send.at[q, role, c], a_recv.at[q, role, c], ahead(q)))

    tgt_copies[1].wait_recv()
    tgt_copies[2].wait_recv()

    def targets(role, i):
        return jnp.broadcast_to(tgt[role, i:i + 1, :], (8, lanes))

    def reduce(role, c, store):
        for q in far:
            a_copies[q, role, c].wait_recv()

        def body(r, carry):
            at = pl.ds(pl.multiple_of(r * 8, 8), 8)
            sums = [jnp.zeros((8, lanes), jnp.float32) for _ in range(OWNB)]
            for q in range(count):
                for s in range(capacity):
                    value = came[c, slot(q, role) + s, at, :]
                    where = targets(role, q * capacity + s)
                    for t in range(OWNB):
                        sums[t] = sums[t] + jnp.where(where == t, value, 0.0)
            for t in range(OWNB):
                store(t, at, r, sums[t])
            return carry

        lax.fori_loop(0, rows // 8, body, 0)

    b_copies = {}

    def answer(role, c, held):
        def body(r, carry):
            at = pl.ds(pl.multiple_of(r * 8, 8), 8)
            values = [held[c, t, at, :] for t in range(OWNB)]
            for q in range(count):
                to = back if q == 0 else ans
                for s in range(capacity):
                    where = targets(role, q * capacity + s)
                    out = values[0]
                    for t in range(1, OWNB):
                        out = jnp.where(where == t, values[t], out)
                    to[c, slot(q, role) + s, at, :] = out
            return carry

        lax.fori_loop(0, rows // 8, body, 0)
        for q in far:
            b_copies[q, role, c] = launch(remote(
                part(ans, c, q, role), part(back, c, q, role),
                b_send.at[q, role, c], b_recv.at[q, role, c], behind(q)))

    y_copies, x_copies, g_copies, h_copies = {}, {}, {}, {}

    def stage_corner(c):
        def store(t, at, r, value):
            pd[c, t, at, :] = value
        reduce(2, c, store)
        y_copies[c] = launch(remote(pd.at[c], ry.at[c], y_send.at[c], y_recv.at[c], near_y))

    def stage_near(c):
        y_copies[c].wait_recv()

        def store(t, at, r, value):
            px[c, t, at, :] = value + ry[c, t, at, :]
        reduce(1, c, store)
        x_copies[c] = launch(remote(px.at[c], rx.at[c], x_send.at[c], x_recv.at[c], near_x))

    def stage_own(c):
        x_copies[c].wait_recv()

        def store(t, at, r, value):
            value = value + rx[c, t, at, :]
            own[c, t, at, :] = value
            owned_ref[t, pl.ds(pl.multiple_of(c * rows + r * 8, 8), 8), :] = value
        reduce(0, c, store)
        g_copies[c] = launch(remote(own.at[c], g1.at[c], g_send.at[c], g_recv.at[c], near_x))
        answer(0, c, own)

    def stage_back_near(c):
        g_copies[c].wait_recv()
        h_copies[c] = launch(remote(g1.at[c], g2.at[c], h_send.at[c], h_recv.at[c], near_y))
        answer(1, c, g1)

    def stage_back_corner(c):
        h_copies[c].wait_recv()
        answer(2, c, g2)

    stages = [stage_corner, stage_near, stage_own, stage_back_near, stage_back_corner]
    steps = [(c + 2 * i, i, c) for i in range(len(stages)) for c in range(chunks)]
    for _, i, c in sorted(steps):
        stages[i](c)

    for copy in b_copies.values():
        copy.wait_recv()

    def gather(n, carry):
        k = key_ref[n]
        for c in range(chunks):
            comb_ref[n, c * rows:(c + 1) * rows, :] = back[c, k]
        return carry

    lax.fori_loop(0, total, gather, 0, unroll=4)
    for copy in sends:
        copy.wait_send()


def on_device(star_residual, patch_inverse, block_owner, block_slot, recv_target):
    nx, ny, nz = lax.axis_size("gx"), lax.axis_size("gy"), lax.axis_size("gz")
    gx, gy, gz = lax.axis_index("gx"), lax.axis_index("gy"), lax.axis_index("gz")
    patch_count, rhs_count, patch_order = star_residual.shape
    block_count = block_owner.shape[1]
    width = patch_order // block_count
    capacity = recv_target.shape[2]
    total = patch_count * block_count
    ly, lz = len(offsets(ny)), len(offsets(nz))
    count = ly * lz
    slots = count * 3 * capacity
    chunks = CHUNKS
    rows = rhs_count // chunks
    owner = block_owner.reshape(-1)
    at_x = offset_index(owner // (ny * nz), gx, nx)
    role = jnp.where((at_x > 0) & (gx % 2 == 1), 3 - at_x, at_x)
    at_y = offset_index(owner // nz % ny, gy, ny)
    at_z = offset_index(owner % nz, gz, nz)
    key = ((at_y * lz + at_z) * 3 + role) * capacity + block_slot.reshape(-1)
    order = jnp.arange(total, dtype=jnp.int32)
    hit = key[None, :] == jnp.arange(slots, dtype=jnp.int32)[:, None]
    src = jnp.sum(jnp.where(hit, order[None, :], 0), axis=1).astype(jnp.int32)

    smem = pl.BlockSpec(memory_space=pltpu.SMEM)
    vmem = pl.BlockSpec(memory_space=pltpu.VMEM)
    anywhere = pl.BlockSpec(memory_space=pl.ANY)
    f32 = jnp.float32
    slotted = pltpu.VMEM((chunks, slots, rows, width), f32)
    targeted = pltpu.VMEM((chunks, OWNB, rows, width), f32)
    dma = pltpu.SemaphoreType.DMA
    owned, comb = pl.pallas_call(
        functools.partial(kernel, (nx, ny, nz, chunks, block_count, capacity)),
        out_shape=(
            jax.ShapeDtypeStruct((OWNB, rhs_count, width), f32),
            jax.ShapeDtypeStruct((total, rhs_count, width), f32),
        ),
        in_specs=[smem, smem, smem, anywhere, anywhere],
        out_specs=(vmem, vmem),
        scratch_shapes=[
            pltpu.VMEM(star_residual.shape, star_residual.dtype),
            pltpu.VMEM((total, width, patch_order), patch_inverse.dtype),
            slotted, slotted,
            pltpu.VMEM((3, count * capacity, width), jnp.int32),
            pltpu.VMEM((3, count * capacity, width), jnp.int32),
            targeted, targeted, targeted, targeted, targeted, targeted, targeted,
            slotted, slotted,
            dma((patch_count + 1,)), dma((2,)), dma((2,)),
            dma((count, 3, chunks)), dma((count, 3, chunks)),
            dma((chunks,)), dma((chunks,)), dma((chunks,)), dma((chunks,)),
            dma((chunks,)), dma((chunks,)), dma((chunks,)), dma((chunks,)),
            dma((count, 3, chunks)), dma((count, 3, chunks)),
        ],
        compiler_params=pltpu.CompilerParams(
            collective_id=0, has_side_effects=True, vmem_limit_bytes=56 * 1024 * 1024),
    )(src, key, recv_target, star_residual,
      patch_inverse.reshape(total, width, patch_order))
    return owned, comb.reshape(patch_count, block_count, rhs_count, width)


def solution(mesh):
    placed = (
        P(("gx", "gy", "gz"), None, None),
        P(("gx", "gy", "gz"), None, None),
        P(("gx", "gy", "gz"), None),
        P(("gx", "gy", "gz"), None),
        P(("gx", "gy", "gz"), None, None),
    )
    return jax.shard_map(
        on_device,
        mesh=mesh,
        in_specs=placed,
        out_specs=(P(("gx", "gy", "gz"), None, None), P(("gx", "gy", "gz"), None, None, None)),
        check_vma=False,
    )
```

time: 155 us -> 56.1 us (0.36)
  waiting for transfers between devices: 100 us -> 0 us
  Pallas kernels: 0 us -> 47.5 us
  starting transfers between devices: 16.2 us -> 0 us
  local copies, waits for them, and re-layouts: 18.3 us -> 6.98 us
  matrix products: 10.9 us -> 0 us
  other arithmetic: 6.95 us -> 0.66 us
    ppermute x12 -> x0, waiting for transfers between devices: 100 us -> none  [from_behind(): lax.ppermute(array, axis, [(i, (i + by) % length) for i in range(length)])]
    pallas_call x0 -> x1, Pallas kernels: none -> 47.5 us  [on_device(): pl.pallas_call(functools.partial(kernel, (nx, ny, nz, chunks, block_count...]
    ppermute x12 -> x0, starting transfers between devices: 16.2 us -> none  [from_behind(): lax.ppermute(array, axis, [(i, (i + by) % length) for i in range(length)])]
    dot_general x5 -> x0, matrix products: 10.9 us -> none  [the longest x1 5.98 us: on_device(): jnp.einsum('prj,pbwj->pbrw', star_residual, inverse_blocks, preferred_ele...]
    concatenate x4 -> x0, other arithmetic: 6.88 us -> none  [move_layers(): jnp.concatenate([lower_move(lower), middle, upper_move(upper)], axis=dim)]
    slice x12 -> x0, local copies, waits for them, and re-layouts: 6.28 us -> none  [the longest x6 2.91 us: move_layers(): lower = lax.index_in_dim(buffer, 0, dim, keepdims=True)]
    reshape x4 -> x2, local copies, waits for them, and re-layouts: 6.62 us -> 1.53 us  [the longest x1 0.76 us: on_device(): owner = block_owner.reshape(-1)]
    unnamed x18 -> x5, local copies, waits for them, and re-layouts: 4.42 us -> 5.45 us
  transfers between devices with their start and end apart: 12 -> 0, of which waited for: 12 -> 0; matrix products, arithmetic and copies ran while one was open for 4% -> 0% of each run, Pallas kernels for 0% -> 0%
where the time goes in v1:
time: 56.1 us; the launch traced here: 55.8 us
  Pallas kernels  47.5 us (85%)
  local copies, waits for them, and re-layouts  6.98 us (12%)
  between operations  0.67 us (1%)
  other arithmetic  0.66 us (1%)
    pallas_call x1, Pallas kernels, on_device(): pl.pallas_call(functools.partial(kernel, (nx, ny, nz, chunks, block_count...  47.5 us
    unnamed x5, local copies, waits for them, and re-layouts  5.45 us

profile of v1, /device:TPU:1, one launch (start us, length us, event | category | flops | bytes accessed | tf_op | source)
XLA Modules:
  0.0 55.8 jit_solution(16372174548338865901)
XLA Ops:
  0.6 0.8 %reshape.141 = s32[36]{0:T(128)S(1)} reshape(s32[4,9]{1,0:T(4,128)} %param.7) | data formatting | bytes 288 | tf_op jit(solution)/shard_map/reshape | solution.py:239
  1.4 0.8 %reshape.142 = s32[36]{0:T(128)S(1)} reshape(s32[4,9]{1,0:T(4,128)} %param.8) | data formatting | bytes 288 | tf_op jit(solution)/shard_map/reshape | solution.py:244
  2.2 0.0 copy-start
  2.2 0.6 %select_reduce_fusion.src_ref = s32[36]{0:T(128)} fusion(s32[36]{0:T(128)S(1)} %multiply_add_fusion.key_ref), kind=kLoop, calls=%fused_computation | loop fusion | flops 3852 | bytes 288 | tf_op jit(solution)/shard_map/reduce_sum | solution.py:247
  2.8 1.4 %copy.8.table_ref = s32[1,27,2]{2,1,0:T(8,128)} copy(s32[1,27,2]{1,2,0:T(2,128)} %param.9) | data formatting | bytes 432 | tf_op args[4]
  4.2 0.0 copy-done
  4.2 47.5 %shard_map.68 = (f32[8,64,128]{2,1,0:T(8,128)}, f32[36,64,128]{2,1,0:T(8,128)}) custom-call(s32[36]{0:T(128)} %select_reduce_fusion.src_ref, s32[36]{0:T(128)} %copy-done, s32[1,27,2]{2,1,0:T(8,128)} %copy.8.table_ref, bf16[4,64,1152]{2,1,0:T(8,128)(2,1)} %star_ref.1, bf16[36,128,1152]{2,1,0:T(8,128)(2,1)} %bitcast.2), custom_call_target="tpu_custom_call" | custom-call | tf_op jit(solution)/shard_map/pallas_call | solution.py:256
  51.7 1.7 %copy.11 = f32[8,64,128]{2,1,0:T(8,128)} copy(f32[8,64,128]{2,1,0:T(8,128)} %get-tuple-element.8) | data formatting | bytes 524288
  53.4 2.4 %copy.12 = f32[4,9,64,128]{3,2,1,0:T(8,128)} copy(f32[4,9,64,128]{3,2,1,0:T(8,128)} %bitcast.3) | data formatting | bytes 2359296
  (1 shorter events, 0.0 us)
Async XLA Ops:
  2.2 2.0 %copy-start = (s32[36]{0:T(128)}, s32[36]{0:T(128)S(1)}, u32[]{:S(2)}) copy-start(s32[36]{0:T(128)S(1)} %multiply_add_fusion.key_ref) | copy-start | bytes 436

commit v2 on v1

--- a/solution.py
+++ b/solution.py
@@ -17,17 +17,52 @@
 
 
 def offset_index(far, near, extent):
-    distance = (far - near) % extent
-    return jnp.where(distance <= 1, distance, 2).astype(jnp.int32)
+    distance = lax.rem(far - near + extent, extent)
+    return jnp.where(distance <= 1, distance, 2)
+
+
+def slot_of(owner, block_slot, extents, capacity):
+    nx, ny, nz = extents
+    gx, gy, gz = lax.axis_index("gx"), lax.axis_index("gy"), lax.axis_index("gz")
+    at_x = offset_index(lax.div(owner, ny * nz), gx, nx)
+    role = jnp.where((at_x > 0) & (lax.rem(gx, 2) == 1), 3 - at_x, at_x)
+    at_y = offset_index(lax.rem(lax.div(owner, nz), ny), gy, ny)
+    at_z = offset_index(lax.rem(owner, nz), gz, nz)
+    return ((at_y * len(offsets(nz)) + at_z) * 3 + role) * capacity + block_slot
 
 
 def code_of(offset):
     return offset + 1
 
 
-def kernel(cfg, src_ref, key_ref, table_ref, star_ref, inv_hbm, owned_ref, comb_ref,
-           star, inv, sent, came, tgt_out, tgt, pd, px, ry, rx, own, g1, g2, ans, back,
-           load_sem, tgt_send, tgt_recv, a_send, a_recv, y_send, y_recv, x_send, x_recv,
+def gather_kernel(cfg, owner_ref, slot_ref, held_ref, back_ref, owned_ref, comb_ref,
+                  own, comb, in_sem, out_sem):
+    extents, capacity = cfg
+    patch_count, block_count = owner_ref.shape
+    own_in = pltpu.make_async_copy(held_ref, own, in_sem.at[patch_count])
+    own_out = pltpu.make_async_copy(own, owned_ref, out_sem.at[patch_count])
+    own_in.start()
+    for p in range(patch_count):
+        def fetch(b, carry):
+            k = slot_of(owner_ref[p, b], slot_ref[p, b], extents, capacity)
+            pltpu.make_async_copy(back_ref.at[k], comb.at[p, b], in_sem.at[p]).start()
+            return carry
+        lax.fori_loop(0, block_count, fetch, 0, unroll=True)
+    own_in.wait()
+    own_out.start()
+    outs = [own_out]
+    for p in range(patch_count):
+        pltpu.make_async_copy(back_ref.at[pl.ds(0, block_count)], comb.at[p], in_sem.at[p]).wait()
+        out = pltpu.make_async_copy(comb.at[p], comb_ref.at[p], out_sem.at[p])
+        out.start()
+        outs.append(out)
+    for out in outs:
+        out.wait()
+
+
+def kernel(cfg, owner_ref, slot_ref, table_ref, star_ref, inv_hbm, owned_ref, back,
+           star, inv, key_ref, src_ref, sent, came, tgt_out, tgt, pd, px, ry, rx, own, g1, g2, ans,
+           own_sem, self_sem, load_sem, tgt_send, tgt_recv, a_send, a_recv, y_send, y_recv, x_send, x_recv,
            g_send, g_recv, h_send, h_recv, b_send, b_recv):
     nx, ny, nz, chunks, block_count, capacity = cfg
     gx, gy, gz = lax.axis_index("gx"), lax.axis_index("gy"), lax.axis_index("gz")
@@ -68,7 +103,23 @@
             code = 9 * code_x + 3 * code_of(pairs[q][0]) + code_of(pairs[q][1])
             for s in range(capacity):
                 i = q * capacity + s
-                held[role, i:i + 1, :] = jnp.full((1, lanes), table_ref[0, code, s], jnp.int32)
+                held[role, i:i + 1, :] = jnp.full((1, lanes), table_ref[0, s, code], jnp.int32)
+
+    def number(n, carry):
+        p, b = lax.div(n, block_count), lax.rem(n, block_count)
+        key_ref[n] = slot_of(owner_ref[p, b], slot_ref[p, b], (nx, ny, nz), capacity)
+        return carry
+
+    lax.fori_loop(0, total, number, 0)
+
+    def invert(k, carry):
+        found = jnp.int32(0)
+        for n in range(total):
+            found = jnp.where(key_ref[n] == k, n, found)
+        src_ref[k] = found
+        return carry
+
+    lax.fori_loop(0, count * 3 * capacity, invert, 0)
 
     pl.semaphore_wait(barrier, len(greeted))
 
@@ -147,25 +198,34 @@
         lax.fori_loop(0, rows // 8, body, 0)
 
     b_copies = {}
+    locals_ = []
+
+    def landing(c, q, role):
+        return back.at[pl.ds(slot(q, role), capacity), pl.ds(c * rows, rows)]
+
+    def put(source, target, sem):
+        copy = pltpu.make_async_copy(source, target, sem)
+        copy.start()
+        locals_.append(copy)
 
     def answer(role, c, held):
         def body(r, carry):
             at = pl.ds(pl.multiple_of(r * 8, 8), 8)
             values = [held[c, t, at, :] for t in range(OWNB)]
             for q in range(count):
-                to = back if q == 0 else ans
                 for s in range(capacity):
                     where = targets(role, q * capacity + s)
                     out = values[0]
                     for t in range(1, OWNB):
                         out = jnp.where(where == t, values[t], out)
-                    to[c, slot(q, role) + s, at, :] = out
+                    ans[c, slot(q, role) + s, at, :] = out
             return carry
 
         lax.fori_loop(0, rows // 8, body, 0)
+        put(part(ans, c, 0, role), landing(c, 0, role), self_sem.at[role, c])
         for q in far:
             b_copies[q, role, c] = launch(remote(
-                part(ans, c, q, role), part(back, c, q, role),
+                part(ans, c, q, role), landing(c, q, role),
                 b_send.at[q, role, c], b_recv.at[q, role, c], behind(q)))
 
     y_copies, x_copies, g_copies, h_copies = {}, {}, {}, {}
@@ -188,11 +248,10 @@
         x_copies[c].wait_recv()
 
         def store(t, at, r, value):
-            value = value + rx[c, t, at, :]
-            own[c, t, at, :] = value
-            owned_ref[t, pl.ds(pl.multiple_of(c * rows + r * 8, 8), 8), :] = value
+            own[c, t, at, :] = value + rx[c, t, at, :]
         reduce(0, c, store)
         g_copies[c] = launch(remote(own.at[c], g1.at[c], g_send.at[c], g_recv.at[c], near_x))
+        put(own.at[c], owned_ref.at[:, pl.ds(c * rows, rows)], own_sem.at[c])
         answer(0, c, own)
 
     def stage_back_near(c):
@@ -212,20 +271,14 @@
     for copy in b_copies.values():
         copy.wait_recv()
 
-    def gather(n, carry):
-        k = key_ref[n]
-        for c in range(chunks):
-            comb_ref[n, c * rows:(c + 1) * rows, :] = back[c, k]
-        return carry
-
-    lax.fori_loop(0, total, gather, 0, unroll=4)
+    for copy in locals_:
+        copy.wait()
     for copy in sends:
         copy.wait_send()
 
 
 def on_device(star_residual, patch_inverse, block_owner, block_slot, recv_target):
     nx, ny, nz = lax.axis_size("gx"), lax.axis_size("gy"), lax.axis_size("gz")
-    gx, gy, gz = lax.axis_index("gx"), lax.axis_index("gy"), lax.axis_index("gz")
     patch_count, rhs_count, patch_order = star_residual.shape
     block_count = block_owner.shape[1]
     width = patch_order // block_count
@@ -236,39 +289,31 @@
     slots = count * 3 * capacity
     chunks = CHUNKS
     rows = rhs_count // chunks
-    owner = block_owner.reshape(-1)
-    at_x = offset_index(owner // (ny * nz), gx, nx)
-    role = jnp.where((at_x > 0) & (gx % 2 == 1), 3 - at_x, at_x)
-    at_y = offset_index(owner // nz % ny, gy, ny)
-    at_z = offset_index(owner % nz, gz, nz)
-    key = ((at_y * lz + at_z) * 3 + role) * capacity + block_slot.reshape(-1)
-    order = jnp.arange(total, dtype=jnp.int32)
-    hit = key[None, :] == jnp.arange(slots, dtype=jnp.int32)[:, None]
-    src = jnp.sum(jnp.where(hit, order[None, :], 0), axis=1).astype(jnp.int32)
-
     smem = pl.BlockSpec(memory_space=pltpu.SMEM)
-    vmem = pl.BlockSpec(memory_space=pltpu.VMEM)
     anywhere = pl.BlockSpec(memory_space=pl.ANY)
     f32 = jnp.float32
     slotted = pltpu.VMEM((chunks, slots, rows, width), f32)
     targeted = pltpu.VMEM((chunks, OWNB, rows, width), f32)
     dma = pltpu.SemaphoreType.DMA
-    owned, comb = pl.pallas_call(
+    held, back = pl.pallas_call(
         functools.partial(kernel, (nx, ny, nz, chunks, block_count, capacity)),
         out_shape=(
             jax.ShapeDtypeStruct((OWNB, rhs_count, width), f32),
-            jax.ShapeDtypeStruct((total, rhs_count, width), f32),
+            jax.ShapeDtypeStruct((slots, rhs_count, width), f32),
         ),
         in_specs=[smem, smem, smem, anywhere, anywhere],
-        out_specs=(vmem, vmem),
+        out_specs=(anywhere, anywhere),
         scratch_shapes=[
             pltpu.VMEM(star_residual.shape, star_residual.dtype),
             pltpu.VMEM((total, width, patch_order), patch_inverse.dtype),
+            pltpu.SMEM((total,), jnp.int32),
+            pltpu.SMEM((slots,), jnp.int32),
             slotted, slotted,
             pltpu.VMEM((3, count * capacity, width), jnp.int32),
             pltpu.VMEM((3, count * capacity, width), jnp.int32),
             targeted, targeted, targeted, targeted, targeted, targeted, targeted,
-            slotted, slotted,
+            slotted,
+            dma((chunks,)), dma((3, chunks)),
             dma((patch_count + 1,)), dma((2,)), dma((2,)),
             dma((count, 3, chunks)), dma((count, 3, chunks)),
             dma((chunks,)), dma((chunks,)), dma((chunks,)), dma((chunks,)),
@@ -277,9 +322,22 @@
         ],
         compiler_params=pltpu.CompilerParams(
             collective_id=0, has_side_effects=True, vmem_limit_bytes=56 * 1024 * 1024),
-    )(src, key, recv_target, star_residual,
+    )(block_owner, block_slot, recv_target.transpose(0, 2, 1), star_residual,
       patch_inverse.reshape(total, width, patch_order))
-    return owned, comb.reshape(patch_count, block_count, rhs_count, width)
+    return pl.pallas_call(
+        functools.partial(gather_kernel, ((nx, ny, nz), capacity)),
+        out_shape=(
+            jax.ShapeDtypeStruct((OWNB, rhs_count, width), f32),
+            jax.ShapeDtypeStruct((patch_count, block_count, rhs_count, width), f32),
+        ),
+        in_specs=[smem, smem, anywhere, anywhere],
+        out_specs=(anywhere, anywhere),
+        scratch_shapes=[
+            pltpu.VMEM((OWNB, rhs_count, width), f32),
+            pltpu.VMEM((patch_count, block_count, rhs_count, width), f32),
+            dma((patch_count + 1,)), dma((patch_count + 1,)),
+        ],
+    )(block_owner, block_slot, held, back)
 
 
 def solution(mesh):

time: 56.1 us -> 50.2 us (0.89)
  local copies, waits for them, and re-layouts: 6.98 us -> 0 us
  Pallas kernels: 47.5 us -> 49.3 us
  other arithmetic: 0.66 us -> 0 us
    unnamed x5 -> x0, local copies, waits for them, and re-layouts: 5.45 us -> none
    pallas_call x0 -> x1, Pallas kernels: none -> 3.01 us  [on_device(): pl.pallas_call(functools.partial(gather_kernel, ((nx, ny, nz), capacity))...]
    reshape x2 -> x0, local copies, waits for them, and re-layouts: 1.53 us -> none  [the longest x1 0.76 us: on_device(): owner = block_owner.reshape(-1)]
    pallas_call x1, Pallas kernels: 47.5 us -> 46.3 us  [on_device(): pl.pallas_call(functools.partial(kernel, (nx, ny, nz, chunks, block_count...]
    reduce_sum x1 -> x0, other arithmetic: 0.63 us -> none  [on_device(): src = jnp.sum(jnp.where(hit, order[None, :], 0), axis=1).astype(jnp.int32)]
where the time goes in v2:
time: 50.2 us; the launch traced here: 49.9 us
  Pallas kernels  49.3 us (98%)
  between operations  0.64 us (1%)
    pallas_call x1, Pallas kernels, on_device(): pl.pallas_call(functools.partial(kernel, (nx, ny, nz, chunks, block_count...  46.3 us
    pallas_call x1, Pallas kernels, on_device(): pl.pallas_call(functools.partial(gather_kernel, ((nx, ny, nz), capacity))...  3.01 us

profile of v2, /device:TPU:1, one launch (start us, length us, event | category | flops | bytes accessed | tf_op | source)
XLA Modules:
  0.0 49.9 jit_solution(4576796447602681531)
XLA Ops:
  0.6 46.3 %shard_map.68 = (f32[8,64,128]{2,1,0:T(8,128)}, f32[36,64,128]{2,1,0:T(8,128)}) custom-call(s32[4,9]{1,0:T(4,128)} %owner_ref.3, s32[4,9]{1,0:T(4,128)} %slot_ref.3, s32[1,2,27]{2,1,0:T(2,128)} %bitcast.3, bf16[4,64,1152]{2,1,0:T(8,128)(2,1)} %star_ref.1, bf16[36,128,1152]{2,1,0:T(8,128)(2,1)} %bitcast.2), custom_call_target="tpu_custom_call" | custom-call | tf_op jit(solution)/shard_map/pallas_call | solution.py:298
  46.9 3.0 %shard_map.69 = (f32[8,64,128]{2,1,0:T(8,128)}, f32[4,9,64,128]{3,2,1,0:T(8,128)}) custom-call(s32[4,9]{1,0:T(4,128)} %owner_ref.3, s32[4,9]{1,0:T(4,128)} %slot_ref.3, f32[8,64,128]{2,1,0:T(8,128)} %get-tuple-element.4.held_ref, f32[36,64,128]{2,1,0:T(8,128)} %get-tuple-element.5.back_ref), custom_call_target="tpu_custom_call" | custom-call | tf_op jit(solution)/shard_map/pallas_call | solution.py:327
